TPU v7x, 32 devices: a whole 2x2x4 slice. The times are simulated.
32 devices in a mesh: ep: 8 (over y, x, core), tp: 4 (over z).
Axes of the slice: x: 2, y: 2, z: 4, core: 2. Of those that a mesh axis runs over, the one named last changes fastest.
Arguments:
- tokens: bfloat16 [256, 4096], P('ep', 'tp'), may hold values from -6 to 6
- norm_gains: float32 [2, 4096], replicated, may hold values from 0.1 to 1.9
- router: bfloat16 [2, 4096, 16], replicated, as said below
- w_gate: bfloat16 [2, 16, 4096, 768], P(None, 'ep', None, 'tp'), may hold values from -0.09375 to 0.09375
- w_up: bfloat16 [2, 16, 4096, 768], P(None, 'ep', None, 'tp'), may hold values from -0.09375 to 0.09375
- w_down: bfloat16 [2, 16, 768, 4096], P(None, 'ep', 'tp'), may hold values from -0.21875 to 0.21875
- expert_ids: int32 [2, 256, 8], P(None, 'ep'), may hold values from 0 to 15, all different within a row; in each aligned block of 32 rows (0 to 31, 32 to 63, ...) at most 32 rows name the same one
Outputs:
- hidden_out: bfloat16 [256, 4096], P('ep', 'tp')
Inputs may be any that keep to these rules, and one draw needn't show every extreme that they name: `expert_ids`: each entry names an expert of 0 to 15; the 8 entries of a token differ; among the 32 tokens of one ep index in one layer no expert is named more than 32 times, and in some such blocks one is named exactly 32 times. `router`: entries of order 2 / sqrt(4096); all columns of a layer may share a common added vector with entries of order 50 / sqrt(4096).
All inputs are finite; a program needn't handle non-finite values.
Results may differ from a plain program's by a relative error of at most 0.02.
Values may be sent and summed in bfloat16 or wider, within the bound.
A program may use at most 64 MiB of HBM per device.

v0:
```python
import jax
import jax.numpy as jnp
from jax import lax
from jax.sharding import PartitionSpec as P

TOP = 8
LAYERS = 2
norm_eps = 1e-06


def body(tokens, norm_gains, router, w_gate, w_up, w_down, expert_ids):
    n_tp = lax.axis_size("tp")
    n_ep = lax.axis_size("ep")
    local_width = tokens.shape[1]
    full_width = local_width * n_tp
    rows_dev = tokens.shape[0]
    local_exp = w_gate.shape[1]
    experts = local_exp * n_ep
    capacity = 2 * rows_dev * TOP // experts
    current = tokens
    for layer_idx in range(LAYERS):
        gain = norm_gains[layer_idx]
        weight = router[layer_idx]
        ids = expert_ids[layer_idx]
        normed = None
        whole = lax.all_gather(current, "tp", axis=1, tiled=True)
        wide_rows = whole.astype(jnp.float32)
        square_sum = jnp.sum(wide_rows * wide_rows, axis=1)
        scaled = (wide_rows * gain[None, :]).astype(jnp.bfloat16)
        raw_logits = jnp.dot(scaled, weight, preferred_element_type=jnp.float32)
        inverse = lax.rsqrt(square_sum / full_width + norm_eps)
        normed = (scaled.astype(jnp.float32) * inverse[:, None]).astype(jnp.bfloat16)
        logits = raw_logits * inverse[:, None]
        choose = ids[:, :, None] == lax.iota(jnp.int32, experts)[None, None, :]
        picked = jnp.sum(jnp.where(choose, logits[:, None, :], 0.0), axis=-1)
        gate_probs = jax.nn.softmax(picked, axis=-1)
        onehot = choose.reshape(rows_dev * TOP, experts).astype(jnp.int32)
        earlier = jnp.cumsum(onehot, axis=0) - onehot
        slot_index = jnp.sum(earlier * onehot, axis=1).reshape(rows_dev, TOP)
        slot_key = ids * capacity + slot_index
        slot_hits = slot_key[None, :, :] == lax.iota(jnp.int32, experts * capacity)[:, None, None]
        route_matrix = jnp.any(slot_hits, axis=-1).astype(jnp.bfloat16)
        combine_matrix = jnp.sum(jnp.where(slot_hits, gate_probs[None, :, :], 0.0), axis=-1).T
        outgoing = jnp.dot(route_matrix, normed, preferred_element_type=jnp.float32).astype(
            jnp.bfloat16
        )
        outgoing = outgoing.reshape(n_ep, local_exp * capacity, full_width)
        incoming = lax.all_to_all(outgoing, "ep", split_axis=0, concat_axis=0, tiled=True)
        arrived = incoming.reshape(n_ep, local_exp, capacity, full_width).transpose(1, 0, 2, 3)
        arrived = arrived.reshape(local_exp, n_ep * capacity, full_width)
        gate_proj = jnp.einsum(
            "erd,edf->erf", arrived, w_gate[layer_idx], preferred_element_type=jnp.float32
        )
        up_proj = jnp.einsum(
            "erd,edf->erf", arrived, w_up[layer_idx], preferred_element_type=jnp.float32
        )
        inner = (jax.nn.silu(gate_proj) * up_proj).astype(jnp.bfloat16)
        down_local = w_down[layer_idx]

        def project():
            down_piece = lax.slice_in_dim(down_local, 0, local_width * lax.axis_size("tp"), axis=2)
            return jnp.einsum("erf,efd->der", inner, down_piece, preferred_element_type=jnp.float32)

        summed = lax.psum_scatter(
            project().astype(jnp.bfloat16), "tp", scatter_dimension=0, tiled=True
        ).astype(jnp.float32)
        out_rows = summed.astype(jnp.bfloat16).reshape(local_width, local_exp, n_ep, capacity)
        out_rows = out_rows.transpose(2, 1, 3, 0).reshape(n_ep, local_exp * capacity, local_width)
        returned = lax.all_to_all(out_rows, "ep", split_axis=0, concat_axis=0, tiled=True)
        returned = returned.reshape(experts * capacity, local_width).astype(jnp.float32)
        moe_out = jnp.dot(combine_matrix, returned, precision=lax.Precision.HIGHEST)
        current = (current.astype(jnp.float32) + moe_out).astype(jnp.bfloat16)
    return current


def solution(mesh):
    in_specs = (
        P("ep", "tp"),
        P(),
        P(),
        P(None, "ep", None, "tp"),
        P(None, "ep", None, "tp"),
        P(None, "ep", "tp", None),
        P(None, "ep", None),
    )
    out_specs = P("ep", "tp")
    return jax.shard_map(body, mesh=mesh, in_specs=in_specs, out_specs=out_specs, check_vma=False)
```

profile of v0, /device:TPU:0, one launch (start us, length us, event | category | flops | bytes accessed | tf_op | source)
XLA Modules:
  0.0 376.2 jit_solution(15348728780867839647)
XLA Ops:
  6.5 0.7 fusion.79
  7.5 0.6 reduce-window.14
  8.5 0.2 fusion.41
  8.8 0.9 fusion.78
  9.6 15.9 %all_gather.6 = bf16[32,4096]{1,0:T(8,128)(2,1)S(1)} all-gather(bf16[32,1024]{1,0:T(8,128)(2,1)} %param.7), channel_id=1, replica_groups=mesh['ep'=8,'tp'=4] {'tp'}, dimensions={1}, use_global_device_ids=true | all-gather | bytes 327680 | tf_op jit(solution)/shard_map/all_gather | solution.py:26
  25.7 1.3 convolution_convert_fusion.3
  27.0 52.8 %all_to_all.20 = bf16[8,64,4096]{2,1,0:T(8,128)(2,1)S(1)} all-to-all(bf16[8,64,4096]{2,1,0:T(8,128)(2,1)S(1)} %bitcast.120), channel_id=1, replica_groups=mesh['ep'=8,'tp'=4] {'ep'}, dimensions={0} | all-to-all | bytes 8388608 | tf_op jit(solution)/shard_map/all_to_all | solution.py:48
  79.8 0.5 copy.30
  80.3 2.0 copy-done
  82.3 1.5 fusion.10
  83.9 8.8 %fusion = bf16[4096,2,256]{0,2,1:T(8,128)(2,1)} fusion(bf16[2,2,192,4096]{3,2,1,0:T(8,128)(2,1)} %param.12, bf16[2,256,4096]{2,1,0:T(8,128)(2,1)} %bitcast.125, bf16[2,2,4096,192]{2,3,1,0:T(8,128)(2,1)} %param.11, f32[2,256,192]{1,2,0:T(8,128)S(1)} %fusion.10), kind=kOutput, calls=%fused_computation.4 | convolution fusion | flops 1613299712 | bytes 15073280 | tf_op jit(solution)/shard_map/erf,efd->der/dot_general | solution.py:62
  92.9 0.6 reduce-window.16
  94.1 75.1 %reduce-scatter.3.cloned.1.call-done = bf16[1024,2,256]{0,2,1:T(8,128)(2,1)} async-done(((bf16[4096,2,256]{0,2,1:T(8,128)(2,1)}), bf16[1024,2,256]{0,2,1:T(8,128)(2,1)}) %reduce-scatter.3.cloned.1.call-update) | async-done | bytes 1048592 | tf_op jit(solution)/shard_map/reduce_scatter | solution.py:64
  169.3 2.3 copy.31
  171.6 3.6 all-to-all-start.1
  175.4 0.2 fusion.40
  175.7 0.2 select_reduce_fusion.1
  175.9 14.7 %all-to-all-done.1 = bf16[8,64,1024]{2,1,0:T(8,128)(2,1)S(1)} async-done(((bf16[8,64,1024]{2,1,0:T(8,128)(2,1)}), bf16[8,64,1024]{2,1,0:T(8,128)(2,1)S(1)}, u32[]{:S(2)}, u32[]{:S(2)}) %all-to-all-start.1) | async-done | bytes 1048608 | tf_op jit(solution)/shard_map/all_to_all | solution.py:69
  190.6 0.6 fusion.30
  191.2 14.4 %all_gather.7 = bf16[32,4096]{1,0:T(8,128)(2,1)S(1)} all-gather(bf16[32,1024]{1,0:T(8,128)(2,1)S(1)} %fusion.30), channel_id=1, replica_groups=mesh['ep'=8,'tp'=4] {'tp'}, dimensions={1}, use_global_device_ids=true | all-gather | bytes 327680 | tf_op jit(solution)/shard_map/all_gather | solution.py:26
  205.8 1.3 convolution_convert_fusion.1
  207.1 51.8 %all_to_all.21 = bf16[8,64,4096]{2,1,0:T(8,128)(2,1)S(1)} all-to-all(bf16[8,64,4096]{2,1,0:T(8,128)(2,1)S(1)} %bitcast.122), channel_id=1, replica_groups=mesh['ep'=8,'tp'=4] {'ep'}, dimensions={0} | all-to-all | bytes 8388608 | tf_op jit(solution)/shard_map/all_to_all | solution.py:48
  258.9 0.5 copy.36
  259.4 2.0 copy-done.1
  261.4 1.5 fusion.5
  262.9 8.8 %fusion.1 = bf16[4096,2,256]{0,2,1:T(8,128)(2,1)} fusion(bf16[2,2,192,4096]{3,2,1,0:T(8,128)(2,1)} %param.12, bf16[2,256,4096]{2,1,0:T(8,128)(2,1)} %bitcast.127, bf16[2,2,4096,192]{2,3,1,0:T(8,128)(2,1)} %param.11, f32[2,256,192]{1,2,0:T(8,128)S(1)} %fusion.5), kind=kOutput, calls=%fused_computation.5 | convolution fusion | flops 1613299712 | bytes 15073280 | tf_op jit(solution)/shard_map/erf,efd->der/dot_general | solution.py:62
  271.7 75.0 %reduce-scatter.5.cloned.1.call-done = bf16[1024,2,256]{0,2,1:T(8,128)(2,1)} async-done(((bf16[4096,2,256]{0,2,1:T(8,128)(2,1)}), bf16[1024,2,256]{0,2,1:T(8,128)(2,1)}) %reduce-scatter.5.cloned.1.call-update) | async-done | bytes 1048592 | tf_op jit(solution)/shard_map/reduce_scatter | solution.py:64
  346.7 2.3 copy.37
  349.0 3.7 all-to-all-start.3
  353.1 0.2 select_reduce_fusion
  353.3 14.8 %all-to-all-done.3 = bf16[8,64,1024]{2,1,0:T(8,128)(2,1)S(1)} async-done(((bf16[8,64,1024]{2,1,0:T(8,128)(2,1)}), bf16[8,64,1024]{2,1,0:T(8,128)(2,1)S(1)}, u32[]{:S(2)}, u32[]{:S(2)}) %all-to-all-start.3) | async-done | bytes 1048608 | tf_op jit(solution)/shard_map/all_to_all | solution.py:69
  368.1 1.2 fusion.31
  (56 shorter events, 2.5 us)
Async XLA Ops:
  6.5 162.8 %reduce-scatter.3.cloned.1.call-start = ((), (), s32[]{:S(2)}) async-start(), calls=%async_computation.6 | async-start | bytes 5242880 | tf_op jit(solution)/shard_map/reduce_scatter | solution.py:64
  27.0 55.3 %slice-start = ((s8[6291456]{0:T(1024)(128)(4,1)}), s8[4194304]{0:T(1024)(128)(4,1)S(1)}, s32[]{:S(2)}) async-start(s8[6291456]{0:T(1024)(128)(4,1)} %bitcast.136), calls=%async_computation.8 | async-start | bytes 8388608
  79.8 2.5 slice-start.1
  80.3 2.0 copy-start
  92.6 1.3 copy-start.3
  92.6 98.0 %copy-start.2 = (bf16[32,1024]{1,0:T(8,128)(2,1)S(1)}, bf16[32,1024]{1,0:T(8,128)(2,1)}, u32[]{:S(2)}) copy-start(bf16[32,1024]{1,0:T(8,128)(2,1)} %param.7) | copy-start | bytes 196612
  171.6 19.0 %all-to-all-start.1 = ((bf16[8,64,1024]{2,1,0:T(8,128)(2,1)}), bf16[8,64,1024]{2,1,0:T(8,128)(2,1)S(1)}, u32[]{:S(2)}, u32[]{:S(2)}) async-start(bf16[8,64,1024]{2,1,0:T(8,128)(2,1)} %bitcast.16), calls=%async_computation.2 | async-start | bytes 2097152 | tf_op jit(solution)/shard_map/all_to_all | solution.py:69
  175.2 171.5 %reduce-scatter.5.cloned.1.call-start = ((), (), s32[]{:S(2)}) async-start(), calls=%async_computation.7 | async-start | bytes 5242880 | tf_op jit(solution)/shard_map/reduce_scatter | solution.py:64
  207.1 54.3 %slice-start.2 = ((s8[6291456]{0:T(1024)(128)(4,1)}), s8[4194304]{0:T(1024)(128)(4,1)S(1)}, s32[]{:S(2)}) async-start(s8[6291456]{0:T(1024)(128)(4,1)} %bitcast.138), calls=%async_computation.10 | async-start | bytes 8388608
  258.9 2.5 slice-start.3
  259.4 2.0 copy-start.1
  349.0 19.0 %all-to-all-start.3 = ((bf16[8,64,1024]{2,1,0:T(8,128)(2,1)}), bf16[8,64,1024]{2,1,0:T(8,128)(2,1)S(1)}, u32[]{:S(2)}, u32[]{:S(2)}) async-start(bf16[8,64,1024]{2,1,0:T(8,128)(2,1)} %bitcast.34), calls=%async_computation.5 | async-start | bytes 2097152 | tf_op jit(solution)/shard_map/all_to_all | solution.py:69
Sparse Core Ops, SparseCore 0:
  92.8 76.4 reduce-scatter.2
  271.8 74.8 reduce-scatter.4
where the time goes:
time: 377 us; the launch traced here: 376 us
  waiting for transfers between devices  180 us (48%)
  blocking collectives  135 us (36%)
  matrix products  25.5 us (7%)
  between operations  13.6 us (4%)
  local copies, waits for them, and re-layouts  12.3 us (3%)
  starting transfers between devices  7.32 us (2%)
    reduce_scatter x2, waiting for transfers between devices, body(): lax.psum_scatter(project().astype(jnp.bfloat16), 'tp', scatter_dimension=...  150 us
    all_to_all x2, blocking collectives, body(): lax.all_to_all(outgoing, 'ep', split_axis=0, concat_axis=0, tiled=True)  105 us
    all_gather x2, blocking collectives, body(): whole = lax.all_gather(current, 'tp', axis=1, tiled=True)  30.2 us
    all_to_all x2, waiting for transfers between devices, body(): lax.all_to_all(out_rows, 'ep', split_axis=0, concat_axis=0, tiled=True)  29.5 us
    dot_general x2, matrix products, project(): jnp.einsum('erf,efd->der', inner, down_piece, preferred_element_type=jnp....  17.6 us
  transfers between devices with their start and end apart: 4, of which 4 were waited for; matrix products, arithmetic and copies ran while one was open for 1% of the time, Pallas kernels for 0%

commit v1 on v0

--- a/solution.py
+++ b/solution.py
@@ -23,7 +23,14 @@
         weight = router[layer_idx]
         ids = expert_ids[layer_idx]
         normed = None
-        whole = lax.all_gather(current, "tp", axis=1, tiled=True)
+        ring = [current]
+        for hop in range(3):
+            ring.append(lax.ppermute(ring[-1], "tp", [(dev, (dev + 1) % 4) for dev in range(4)]))
+        whole = jnp.roll(
+            jnp.concatenate(ring[::-1], axis=1),
+            (lax.axis_index("tp") + 1) * ring[0].shape[1],
+            axis=1,
+        )
         wide_rows = whole.astype(jnp.float32)
         square_sum = jnp.sum(wide_rows * wide_rows, axis=1)
         scaled = (wide_rows * gain[None, :]).astype(jnp.bfloat16)

time: 377 us -> 379 us (level)
  blocking collectives: 135 us -> 105 us
  waiting for transfers between devices: 180 us -> 205 us
  starting transfers between devices: 7.32 us -> 12.2 us
    all_gather x2 -> x0, blocking collectives: 30.2 us -> none  [body(): whole = lax.all_gather(current, 'tp', axis=1, tiled=True)]
    ppermute x0 -> x6, waiting for transfers between devices: none -> 30.2 us  [body(): lax.ppermute(ring[-1], 'tp', [(dev, (dev + 1) % 4) for dev in range(4)])]
    ppermute x0 -> x6, starting transfers between devices: none -> 4.81 us  [body(): lax.ppermute(ring[-1], 'tp', [(dev, (dev + 1) % 4) for dev in range(4)])]
    reduce_scatter x2, waiting for transfers between devices: 150 us -> 146 us  [body(): lax.psum_scatter(project().astype(jnp.bfloat16), 'tp', scatter_dimension=...]
  transfers between devices with their start and end apart: 4 -> 10, of which waited for: 4 -> 10; matrix products, arithmetic and copies ran while one was open for 1% -> 2% of each run, Pallas kernels for 0% -> 0%
where the time goes in v1:
time: 379 us
  waiting for transfers between devices  205 us (54%)
  blocking collectives  105 us (28%)
  matrix products  25.5 us (7%)
  between operations  13.6 us (4%)
  local copies, waits for them, and re-layouts  12.3 us (3%)
  starting transfers between devices  12.2 us (3%)
  other arithmetic  5.04 us (1%)
    reduce_scatter x2, waiting for transfers between devices, body(): lax.psum_scatter(project().astype(jnp.bfloat16), 'tp', scatter_dimension=...  146 us
    all_to_all x2, blocking collectives, body(): lax.all_to_all(outgoing, 'ep', split_axis=0, concat_axis=0, tiled=True)  105 us
    ppermute x6, waiting for transfers between devices, body(): lax.ppermute(ring[-1], 'tp', [(dev, (dev + 1) % 4) for dev in range(4)])  30.2 us
    all_to_all x2, waiting for transfers between devices, body(): lax.all_to_all(out_rows, 'ep', split_axis=0, concat_axis=0, tiled=True)  29.3 us
    dot_general x2, matrix products, project(): jnp.einsum('erf,efd->der', inner, down_piece, preferred_element_type=jnp....  17.6 us
  transfers between devices with their start and end apart: 10, of which 10 were waited for; matrix products, arithmetic and copies ran while one was open for 2% of the time, Pallas kernels for 0%

profile of v1, /device:TPU:0, one launch (start us, length us, event | category | flops | bytes accessed | tf_op | source)
XLA Modules:
  0.0 378.6 jit_solution(17621679789536355626)
XLA Ops:
  6.5 3.1 collective-permute-start
  9.6 0.7 fusion.95
  11.4 0.9 fusion.94
  12.4 1.6 collective-permute-done
  14.1 6.0 %collective-permute-done.1 = bf16[32,1024]{1,0:T(8,128)(2,1)S(1)} collective-permute-done((bf16[32,1024]{1,0:T(8,128)(2,1)S(1)}, bf16[32,1024]{1,0:T(8,128)(2,1)S(1)}, u32[]{:S(2)}, u32[]{:S(2)}) %collective-permute-start.1) | collective-permute-done | bytes 65568 | tf_op jit(solution)/shard_map/ppermute | solution.py:28
  20.4 5.8 %collective-permute-done.2 = bf16[32,1024]{1,0:T(8,128)(2,1)S(1)} collective-permute-done((bf16[32,1024]{1,0:T(8,128)(2,1)S(1)}, bf16[32,1024]{1,0:T(8,128)(2,1)S(1)}, u32[]{:S(2)}, u32[]{:S(2)}) %collective-permute-start.2) | collective-permute-done | bytes 65568 | tf_op jit(solution)/shard_map/ppermute | solution.py:28
  26.2 1.6 fusion.37
  27.8 1.3 convolution_convert_fusion.3
  29.1 53.0 %all_to_all.20 = bf16[8,64,4096]{2,1,0:T(8,128)(2,1)S(1)} all-to-all(bf16[8,64,4096]{2,1,0:T(8,128)(2,1)S(1)} %bitcast.120), channel_id=1, replica_groups=mesh['ep'=8,'tp'=4] {'ep'}, dimensions={0} | all-to-all | bytes 8388608 | tf_op jit(solution)/shard_map/all_to_all | solution.py:55
  82.7 2.0 copy-done
  84.6 1.5 fusion.10
  86.2 8.8 %fusion = bf16[4096,2,256]{0,2,1:T(8,128)(2,1)} fusion(bf16[2,2,192,4096]{3,2,1,0:T(8,128)(2,1)} %param.14, bf16[2,256,4096]{2,1,0:T(8,128)(2,1)} %bitcast.125, bf16[2,2,4096,192]{2,3,1,0:T(8,128)(2,1)} %param.13, f32[2,256,192]{1,2,0:T(8,128)S(1)} %fusion.10), kind=kOutput, calls=%fused_computation.4 | convolution fusion | flops 1613299712 | bytes 15073280 | tf_op jit(solution)/shard_map/erf,efd->der/dot_general | solution.py:69
  95.8 72.4 %reduce-scatter.3.cloned.1.call-done = bf16[1024,2,256]{0,2,1:T(8,128)(2,1)} async-done(((bf16[4096,2,256]{0,2,1:T(8,128)(2,1)}), bf16[1024,2,256]{0,2,1:T(8,128)(2,1)}) %reduce-scatter.3.cloned.1.call-update) | async-done | bytes 1048592 | tf_op jit(solution)/shard_map/reduce_scatter | solution.py:71
  168.3 2.3 copy.31
  170.6 3.7 all-to-all-start.1
  175.1 14.5 %all-to-all-done.1 = bf16[8,64,1024]{2,1,0:T(8,128)(2,1)S(1)} async-done(((bf16[8,64,1024]{2,1,0:T(8,128)(2,1)}), bf16[8,64,1024]{2,1,0:T(8,128)(2,1)S(1)}, u32[]{:S(2)}, u32[]{:S(2)}) %all-to-all-start.1) | async-done | bytes 1048608 | tf_op jit(solution)/shard_map/all_to_all | solution.py:76
  189.6 0.6 fusion.30
  190.2 1.5 collective-permute-start.3
  191.9 4.4 %collective-permute-done.3 = bf16[32,1024]{1,0:T(8,128)(2,1)S(1)} collective-permute-done((bf16[32,1024]{1,0:T(8,128)(2,1)S(1)}, bf16[32,1024]{1,0:T(8,128)(2,1)S(1)}, u32[]{:S(2)}, u32[]{:S(2)}) %collective-permute-start.3) | collective-permute-done | bytes 65568 | tf_op jit(solution)/shard_map/ppermute | solution.py:28
  196.6 6.4 %collective-permute-done.4 = bf16[32,1024]{1,0:T(8,128)(2,1)S(1)} collective-permute-done((bf16[32,1024]{1,0:T(8,128)(2,1)S(1)}, bf16[32,1024]{1,0:T(8,128)(2,1)S(1)}, u32[]{:S(2)}, u32[]{:S(2)}) %collective-permute-start.4) | collective-permute-done | bytes 65568 | tf_op jit(solution)/shard_map/ppermute | solution.py:28
  203.2 5.8 %collective-permute-done.5 = bf16[32,1024]{1,0:T(8,128)(2,1)S(1)} collective-permute-done((bf16[32,1024]{1,0:T(8,128)(2,1)S(1)}, bf16[32,1024]{1,0:T(8,128)(2,1)S(1)}, u32[]{:S(2)}, u32[]{:S(2)}) %collective-permute-start.5) | collective-permute-done | bytes 65568 | tf_op jit(solution)/shard_map/ppermute | solution.py:28
  209.0 0.9 fusion.39
  210.0 1.3 convolution_convert_fusion.1
  211.3 51.8 %all_to_all.21 = bf16[8,64,4096]{2,1,0:T(8,128)(2,1)S(1)} all-to-all(bf16[8,64,4096]{2,1,0:T(8,128)(2,1)S(1)} %bitcast.122), channel_id=1, replica_groups=mesh['ep'=8,'tp'=4] {'ep'}, dimensions={0} | all-to-all | bytes 8388608 | tf_op jit(solution)/shard_map/all_to_all | solution.py:55
  263.6 2.0 copy-done.1
  265.6 1.5 fusion.5
  267.1 8.8 %fusion.1 = bf16[4096,2,256]{0,2,1:T(8,128)(2,1)} fusion(bf16[2,2,192,4096]{3,2,1,0:T(8,128)(2,1)} %param.14, bf16[2,256,4096]{2,1,0:T(8,128)(2,1)} %bitcast.127, bf16[2,2,4096,192]{2,3,1,0:T(8,128)(2,1)} %param.13, f32[2,256,192]{1,2,0:T(8,128)S(1)} %fusion.5), kind=kOutput, calls=%fused_computation.5 | convolution fusion | flops 1613299712 | bytes 15073280 | tf_op jit(solution)/shard_map/erf,efd->der/dot_general | solution.py:69
  275.9 73.3 %reduce-scatter.5.cloned.1.call-done = bf16[1024,2,256]{0,2,1:T(8,128)(2,1)} async-done(((bf16[4096,2,256]{0,2,1:T(8,128)(2,1)}), bf16[1024,2,256]{0,2,1:T(8,128)(2,1)}) %reduce-scatter.5.cloned.1.call-update) | async-done | bytes 1048592 | tf_op jit(solution)/shard_map/reduce_scatter | solution.py:71
  349.2 2.3 copy.37
  351.5 3.7 all-to-all-start.3
  355.7 14.8 %all-to-all-done.3 = bf16[8,64,1024]{2,1,0:T(8,128)(2,1)S(1)} async-done(((bf16[8,64,1024]{2,1,0:T(8,128)(2,1)}), bf16[8,64,1024]{2,1,0:T(8,128)(2,1)S(1)}, u32[]{:S(2)}, u32[]{:S(2)}) %all-to-all-start.3) | async-done | bytes 1048608 | tf_op jit(solution)/shard_map/all_to_all | solution.py:76
  370.5 1.2 fusion.31
  (66 shorter events, 5.4 us)
Async XLA Ops:
  6.5 161.7 %reduce-scatter.3.cloned.1.call-start = ((), (), s32[]{:S(2)}) async-start(), calls=%async_computation.6 | async-start | bytes 5242880 | tf_op jit(solution)/shard_map/reduce_scatter | solution.py:71
  6.5 7.5 %collective-permute-start = (bf16[32,1024]{1,0:T(8,128)(2,1)}, bf16[32,1024]{1,0:T(8,128)(2,1)S(1)}, u32[]{:S(2)}, u32[]{:S(2)}) collective-permute-start(bf16[32,1024]{1,0:T(8,128)(2,1)} %param.9), channel_id=1, source_target_pairs={{0,1},{1,2},{2,3},{3,0},{4,5},{5,6},{6,7},{7,4},{8,9},{9,10},{10,1... | collective-permute-start | bytes 196616 | tf_op jit(solution)/shard_map/ppermute | solution.py:28
  14.1 6.1 %collective-permute-start.1 = (bf16[32,1024]{1,0:T(8,128)(2,1)S(1)}, bf16[32,1024]{1,0:T(8,128)(2,1)S(1)}, u32[]{:S(2)}, u32[]{:S(2)}) collective-permute-start(bf16[32,1024]{1,0:T(8,128)(2,1)S(1)} %collective-permute-done), channel_id=1, source_target_pairs={{0,1},{1,2},{2,3},{3,0},{4,5},{5,6},{6,7},{7,4},{8,9},{9,10},{10,1... | collective-permute-start | bytes 196616 | tf_op jit(solution)/shard_map/ppermute | solution.py:28
  20.1 6.1 %collective-permute-start.2 = (bf16[32,1024]{1,0:T(8,128)(2,1)S(1)}, bf16[32,1024]{1,0:T(8,128)(2,1)S(1)}, u32[]{:S(2)}, u32[]{:S(2)}) collective-permute-start(bf16[32,1024]{1,0:T(8,128)(2,1)S(1)} %collective-permute-done.1), channel_id=1, source_target_pairs={{0,1},{1,2},{2,3},{3,0},{4,5},{5,6},{6,7},{7,4},{8,9},{9,10},{10,1... | collective-permute-start | bytes 196616 | tf_op jit(solution)/shard_map/ppermute | solution.py:28
  29.1 55.5 %slice-start = ((s8[6291456]{0:T(1024)(128)(4,1)}), s8[4194304]{0:T(1024)(128)(4,1)S(1)}, s32[]{:S(2)}) async-start(s8[6291456]{0:T(1024)(128)(4,1)} %bitcast.136), calls=%async_computation.8 | async-start | bytes 8388608
  82.2 2.5 slice-start.1
  82.6 2.0 copy-start
  95.0 79.6 %copy-start.3 = (bf16[2,4096,16]{1,2,0:T(8,128)(2,1)S(1)}, bf16[2,4096,16]{1,2,0:T(8,128)(2,1)}, u32[]{:S(2)}) copy-start(bf16[2,4096,16]{1,2,0:T(8,128)(2,1)} %param.11) | copy-start | bytes 786436
  95.0 94.7 %copy-start.2 = (bf16[32,1024]{1,0:T(8,128)(2,1)S(1)}, bf16[32,1024]{1,0:T(8,128)(2,1)}, u32[]{:S(2)}) copy-start(bf16[32,1024]{1,0:T(8,128)(2,1)} %param.9) | copy-start | bytes 196612
  170.6 19.0 %all-to-all-start.1 = ((bf16[8,64,1024]{2,1,0:T(8,128)(2,1)}), bf16[8,64,1024]{2,1,0:T(8,128)(2,1)S(1)}, u32[]{:S(2)}, u32[]{:S(2)}) async-start(bf16[8,64,1024]{2,1,0:T(8,128)(2,1)} %bitcast.16), calls=%async_computation.2 | async-start | bytes 2097152 | tf_op jit(solution)/shard_map/all_to_all | solution.py:76
  174.2 175.0 %reduce-scatter.5.cloned.1.call-start = ((), (), s32[]{:S(2)}) async-start(), calls=%async_computation.7 | async-start | bytes 5242880 | tf_op jit(solution)/shard_map/reduce_scatter | solution.py:71
  190.2 6.1 %collective-permute-start.3 = (bf16[32,1024]{1,0:T(8,128)(2,1)S(1)}, bf16[32,1024]{1,0:T(8,128)(2,1)S(1)}, u32[]{:S(2)}, u32[]{:S(2)}) collective-permute-start(bf16[32,1024]{1,0:T(8,128)(2,1)S(1)} %fusion.30), channel_id=1, source_target_pairs={{0,1},{1,2},{2,3},{3,0},{4,5},{5,6},{6,7},{7,4},{8,9},{9,10},{10,1... | collective-permute-start | bytes 196616 | tf_op jit(solution)/shard_map/ppermute | solution.py:28
  196.3 6.6 %collective-permute-start.4 = (bf16[32,1024]{1,0:T(8,128)(2,1)S(1)}, bf16[32,1024]{1,0:T(8,128)(2,1)S(1)}, u32[]{:S(2)}, u32[]{:S(2)}) collective-permute-start(bf16[32,1024]{1,0:T(8,128)(2,1)S(1)} %collective-permute-done.3), channel_id=1, source_target_pairs={{0,1},{1,2},{2,3},{3,0},{4,5},{5,6},{6,7},{7,4},{8,9},{9,10},{10,1... | collective-permute-start | bytes 196616 | tf_op jit(solution)/shard_map/ppermute | solution.py:28
  203.0 6.1 %collective-permute-start.5 = (bf16[32,1024]{1,0:T(8,128)(2,1)S(1)}, bf16[32,1024]{1,0:T(8,128)(2,1)S(1)}, u32[]{:S(2)}, u32[]{:S(2)}) collective-permute-start(bf16[32,1024]{1,0:T(8,128)(2,1)S(1)} %collective-permute-done.4), channel_id=1, source_target_pairs={{0,1},{1,2},{2,3},{3,0},{4,5},{5,6},{6,7},{7,4},{8,9},{9,10},{10,1... | collective-permute-start | bytes 196616 | tf_op jit(solution)/shard_map/ppermute | solution.py:28
  211.3 54.3 %slice-start.2 = ((s8[6291456]{0:T(1024)(128)(4,1)}), s8[4194304]{0:T(1024)(128)(4,1)S(1)}, s32[]{:S(2)}) async-start(s8[6291456]{0:T(1024)(128)(4,1)} %bitcast.138), calls=%async_computation.10 | async-start | bytes 8388608
  263.1 2.5 slice-start.3
  263.6 2.0 copy-start.1
  351.5 19.0 %all-to-all-start.3 = ((bf16[8,64,1024]{2,1,0:T(8,128)(2,1)}), bf16[8,64,1024]{2,1,0:T(8,128)(2,1)S(1)}, u32[]{:S(2)}, u32[]{:S(2)}) async-start(bf16[8,64,1024]{2,1,0:T(8,128)(2,1)} %bitcast.34), calls=%async_computation.5 | async-start | bytes 2097152 | tf_op jit(solution)/shard_map/all_to_all | solution.py:76
Sparse Core Ops, SparseCore 0:
  95.1 73.1 reduce-scatter.2
  276.1 73.0 reduce-scatter.4
